TPU v7x, 32 devices: a whole 2x2x4 slice. The times are simulated.
32 devices in a mesh: batch: 2 (over x), py: 4 (over z), px: 4 (over y, core).
Axes of the slice: x: 2, y: 2, z: 4, core: 2. Of those that a mesh axis runs over, the one named last changes fastest.
Arguments:
- pair_rep: bfloat16 [1024, 512, 128], P(('batch', 'px'), 'py'), parts along dimension 0
- pair_mask: int32 [1024, 512], P(('batch', 'px'), 'py'), parts along dimension 0
- ln_in: bfloat16 [2, 2, 128], replicated
- w_in: bfloat16 [2, 128, 640], replicated
- b_in: bfloat16 [2, 640], replicated
- ln_out: bfloat16 [2, 2, 128], replicated
- w_out: bfloat16 [2, 128, 128], replicated
- b_out: bfloat16 [2, 128], replicated
Outputs:
- output: bfloat16 [1024, 512, 128], P(('batch', 'px'), 'py'), parts along dimension 0
There are 2 independent parts. A program takes and returns all parts, laid end to end along the dimension named above; an argument that names none is the same for every part.
All inputs are finite; a program needn't handle non-finite values.
Results may differ from a plain program's by a relative error of at most 0.00725319.
Values are sent between devices in bfloat16 or wider.
A program may use at most 1 GiB of HBM per device.

v0:
```python
import jax
import jax.numpy as jnp
from jax import lax
from jax.sharding import PartitionSpec as P

LN_EPS = 1e-5


def layer_norm(values, ln_gain, ln_shift, norm_axis):
    average = jnp.mean(values, axis=norm_axis, keepdims=True)
    centered = values - average
    variance = jnp.mean(centered * centered, axis=norm_axis, keepdims=True)
    return centered * lax.rsqrt(variance + LN_EPS) * ln_gain + ln_shift


def gated_operands(pair_blk, mask_blk, ln_in, w_in, b_in):
    hidden = (w_in.shape[1] - w_in.shape[0]) // 4
    proj_width = 4 * hidden
    normed = layer_norm(pair_blk.astype(jnp.float32), ln_in[0].astype(jnp.float32), ln_in[1].astype(jnp.float32), -1).astype(jnp.bfloat16)
    projected = jnp.einsum('ijd,de->eij', normed, w_in[:, :proj_width], preferred_element_type=jnp.float32)
    projected = projected + b_in[:proj_width].astype(jnp.float32)[:, None, None]
    mask_f32 = mask_blk.astype(jnp.float32)[None]
    left_op = (mask_f32 * jax.nn.sigmoid(projected[:hidden]) * projected[hidden:2 * hidden]).astype(jnp.bfloat16)
    right_op = (mask_f32 * jax.nn.sigmoid(projected[2 * hidden:3 * hidden]) * projected[3 * hidden:]).astype(jnp.bfloat16)
    gate_val = jax.nn.sigmoid(jnp.einsum('ijd,de->ije', normed, w_in[:, proj_width:], preferred_element_type=jnp.float32) + b_in[proj_width:].astype(jnp.float32))
    return left_op, right_op, gate_val


def finish_update(pair_blk, tri_sum, gate_val, ln_out, w_out, b_out):
    normed_sum = layer_norm(tri_sum, ln_out[0].astype(jnp.float32)[:, None, None], ln_out[1].astype(jnp.float32)[:, None, None], 0).astype(jnp.bfloat16)
    update = jnp.einsum('cij,cd->ijd', normed_sum, w_out, preferred_element_type=jnp.float32) + b_out.astype(jnp.float32)
    return (pair_blk.astype(jnp.float32) + gate_val * update).astype(jnp.bfloat16)


def outgoing_sum(left_op, right_op):
    left_rows = lax.all_gather(left_op, 'py', axis=2, tiled=True)
    right_cols = lax.all_gather(right_op, 'px', axis=1, tiled=True)
    right_rows = lax.all_to_all(right_cols, 'py', 1, 2, tiled=True)
    return jnp.einsum('cik,cjk->cij', left_rows, right_rows, preferred_element_type=jnp.float32)


def incoming_sum(left_op, right_op):
    left_rows = lax.all_gather(left_op, 'py', axis=2, tiled=True)
    left_cols = lax.all_to_all(left_rows, 'px', 2, 1, tiled=True)
    right_cols = lax.all_gather(right_op, 'px', axis=1, tiled=True)
    return jnp.einsum('cki,ckj->cij', left_cols, right_cols, preferred_element_type=jnp.float32)


def solution(mesh):
    pair_spec = P(('batch', 'px'), 'py', None)
    mask_spec = P(('batch', 'px'), 'py')
    whole = P()

    def device_body(pair_blk, mask_blk, ln_in, w_in, b_in, ln_out, w_out, b_out):
        for update_idx in range(2):
            left_op, right_op, gate_val = gated_operands(pair_blk, mask_blk, ln_in[update_idx], w_in[update_idx], b_in[update_idx])
            if update_idx == 0:
                tri_sum = outgoing_sum(left_op, right_op)
            else:
                tri_sum = incoming_sum(left_op, right_op)
            pair_blk = finish_update(pair_blk, tri_sum, gate_val, ln_out[update_idx], w_out[update_idx], b_out[update_idx])
        return pair_blk

    return jax.shard_map(device_body, mesh=mesh, in_specs=(pair_spec, mask_spec, whole, whole, whole, whole, whole, whole), out_specs=pair_spec, check_vma=False)
```

profile of v0, /device:TPU:26, one launch (start us, length us, event | category | flops | bytes accessed | tf_op | source)
XLA Modules:
  0.0 1735.5 jit_solution(10373773410867205445)
XLA Ops:
  7.4 6.4 copy.29
  21.4 15.8 fusion.39
  37.2 36.2 %copy.35 = f32[128,128,512]{0,1,2:T(8,128)} copy(f32[128,128,512]{2,1,0:T(8,128)} %fusion.39) | data formatting | bytes 67108864 | tf_op jit(solution)/shard_map/ijd,de->eij/dot_general | solution.py:20
  73.5 23.1 %add_bitcast_fusion.1 = f32[512,128,128]{1,2,0:T(8,128)} fusion(f32[128,128,512]{0,1,2:T(8,128)} %copy.35, f32[512]{0:T(512)S(1)} %bitcast.88), kind=kLoop, calls=%fused_computation.1 | loop fusion | flops 8388608 | bytes 67110912 | tf_op jit(solution)/shard_map/add | solution.py:21
  96.6 16.0 fusion.24
  112.5 110.3 %all-gather.7.cloned.1.call-done = bf16[128,512,128]{1,2,0:T(8,128)(2,1)} async-done(((bf16[128,128,128]{1,2,0:T(8,128)(2,1)}), bf16[128,512,128]{1,2,0:T(8,128)(2,1)}) %all-gather.7.cloned.1.call-update) | async-done | bytes 16777232 | tf_op jit(solution)/shard_map/all_gather | solution.py:37
  222.9 23.7 %copy.36 = bf16[128,512,128]{2,0,1:T(8,128)(2,1)} copy(bf16[128,512,128]{1,2,0:T(8,128)(2,1)} %all-gather.7.cloned.1.call-done) | data formatting | bytes 33554432 | tf_op jit(solution)/shard_map/all_gather | solution.py:37
  246.5 7.6 all-to-all-start
  256.1 628.9 %all-to-all-done = bf16[128,512,128]{2,0,1:T(8,128)(2,1)} async-done(((bf16[128,512,128]{2,0,1:T(8,128)(2,1)}), bf16[128,512,128]{2,0,1:T(8,128)(2,1)}, u32[]{:S(2)}, u32[]{:S(2)}) %all-to-all-start) | async-done | bytes 16777248 | tf_op jit(solution)/shard_map/all_to_all | solution.py:38
  885.0 22.0 %copy.70 = bf16[128,4,128,128]{3,1,2,0:T(4,128)(2,1)} copy(bf16[128,4,128,128]{3,0,2,1:T(8,128)(2,1)} %bitcast.8) | data formatting | bytes 33554432 | tf_op jit(solution)/shard_map/all_to_all | solution.py:38
  907.0 24.9 %all_to_all.29 = bf16[128,128,512]{2,1,0:T(8,128)(2,1)} reshape(bf16[128,128,4,128]{3,2,1,0:T(4,128)(2,1)} %bitcast.82) | data formatting | bytes 33554432 | tf_op jit(solution)/shard_map/all_to_all | solution.py:38
  931.9 15.9 fusion.48
  966.0 13.5 fusion.38
  979.4 36.1 %copy.44 = f32[128,128,512]{0,1,2:T(8,128)} copy(f32[128,128,512]{2,1,0:T(8,128)} %fusion.38) | data formatting | bytes 67108864 | tf_op jit(solution)/shard_map/ijd,de->eij/dot_general | solution.py:20
  1015.6 23.1 %add_bitcast_fusion = f32[512,128,128]{1,2,0:T(8,128)} fusion(f32[128,128,512]{0,1,2:T(8,128)} %copy.44, f32[512]{0:T(512)S(1)} %bitcast.87), kind=kLoop, calls=%fused_computation | loop fusion | flops 8388608 | bytes 67110912 | tf_op jit(solution)/shard_map/add | solution.py:21
  1038.6 16.0 fusion.14
  1055.2 284.4 %all-gather.9.cloned.1.call-done = bf16[128,128,512]{1,2,0:T(8,128)(2,1)} async-done(((bf16[128,128,128]{1,2,0:T(8,128)(2,1)}), bf16[128,128,512]{1,2,0:T(8,128)(2,1)}) %all-gather.9.cloned.1.call-update) | async-done | bytes 16777232 | tf_op jit(solution)/shard_map/all_gather | solution.py:43
  1339.6 14.8 copy.45
  1354.4 272.3 %all_to_all.36 = bf16[128,128,512]{1,0,2:T(8,128)(2,1)S(1)} all-to-all(bf16[128,128,512]{1,0,2:T(8,128)(2,1)S(1)} %copy.45), channel_id=1, replica_groups=mesh['batch'=2,'py'=4,'px'=4] {'px'}, dimensions={2} | all-to-all | bytes 33554432 | tf_op jit(solution)/shard_map/all_to_all | solution.py:44
  1626.7 36.0 %copy.69 = bf16[128,128,4,128]{1,2,3,0:T(4,128)(2,1)} copy(bf16[128,128,4,128]{1,0,3,2:T(8,128)(2,1)S(1)} %bitcast.83) | data formatting | bytes 33554432 | tf_op jit(solution)/shard_map/all_to_all | solution.py:44
  1662.7 24.9 %all_to_all.33 = bf16[128,512,128]{1,2,0:T(8,128)(2,1)} reshape(bf16[128,4,128,128]{2,1,3,0:T(4,128)(2,1)} %bitcast.84) | data formatting | bytes 33554432 | tf_op jit(solution)/shard_map/all_to_all | solution.py:44
  1687.6 16.3 fusion.49
  1714.7 6.3 fusion.13
  1721.1 6.4 copy.50
  (68 shorter events, 39.0 us)
Async XLA Ops:
  7.4 13.8 copy-start.9
  7.4 13.8 copy-start.5
  7.4 215.5 %all-gather.7.cloned.1.call-start = ((), (), s32[]{:S(2)}) async-start(), calls=%async_computation.3 | async-start | bytes 20971520 | tf_op jit(solution)/shard_map/all_gather | solution.py:37
  37.2 36.2 %copy-start.8 = (bf16[2,640]{1,0:T(2,128)(2,1)S(1)}, bf16[2,640]{1,0:T(2,128)(2,1)}, u32[]{:S(2)}) copy-start(bf16[2,640]{1,0:T(2,128)(2,1)} %param.12) | copy-start | bytes 7684
  37.2 36.2 %copy-start.7 = (s32[128,128]{1,0:T(8,128)S(1)}, s32[128,128]{1,0:T(8,128)}, u32[]{:S(2)}) copy-start(s32[128,128]{1,0:T(8,128)} %param.9) | copy-start | bytes 196612
  246.5 8.4 copy-start.10
  246.5 8.9 copy-start.13
  246.5 638.5 %all-to-all-start = ((bf16[128,512,128]{2,0,1:T(8,128)(2,1)}), bf16[128,512,128]{2,0,1:T(8,128)(2,1)}, u32[]{:S(2)}, u32[]{:S(2)}) async-start(bf16[128,512,128]{2,0,1:T(8,128)(2,1)} %copy.36), calls=%async_computation | async-start | bytes 33554432 | tf_op jit(solution)/shard_map/all_to_all | solution.py:38
  254.1 677.8 %all-gather.5.cloned.1.call-start = ((), (), s32[]{:S(2)}) async-start(), calls=%async_computation.2 | async-start | bytes 20971520 | tf_op jit(solution)/shard_map/all_gather | solution.py:36
  254.7 1084.9 %all-gather.9.cloned.1.call-start = ((), (), s32[]{:S(2)}) async-start(), calls=%async_computation.4 | async-start | bytes 20971520 | tf_op jit(solution)/shard_map/all_gather | solution.py:43
  947.8 5.8 copy-start.1
  952.2 3.1 copy-start.6
  955.3 3.2 copy-start.2
  963.9 2.0 copy-start.3
  1054.6 633.0 %all-gather.11.cloned.1.call-start = ((), (), s32[]{:S(2)}) async-start(), calls=%async_computation.5 | async-start | bytes 20971520 | tf_op jit(solution)/shard_map/all_gather | solution.py:45
  1703.9 5.8 copy-start
  1703.9 5.8 copy-start.11
  1703.9 5.8 copy-start.12
  1711.5 3.2 copy-start.4
  1711.5 3.2 copy-start.14
  1711.5 3.2 copy-start.15
Sparse Core Ops, SparseCore 0:
  112.7 110.1 all-gather.6
Sparse Core Ops, SparseCore 1:
  256.2 600.6 all-gather.4
  1054.7 284.9 all-gather.8
  1341.1 196.4 all-gather.10
where the time goes:
time: 1750 us; the launch traced here: 1740 us
  waiting for transfers between devices  1020 us (58%)
  blocking collectives  272 us (16%)
  local copies, waits for them, and re-layouts  234 us (13%)
  other arithmetic  101 us (6%)
  matrix products  79.5 us (5%)
    all_to_all x1, waiting for transfers between devices, outgoing_sum(): right_rows = lax.all_to_all(right_cols, 'py', 1, 2, tiled=True)  629 us
    all_gather x1, waiting for transfers between devices, incoming_sum(): left_rows = lax.all_gather(left_op, 'py', axis=2, tiled=True)  284 us
    all_to_all x1, blocking collectives, incoming_sum(): left_cols = lax.all_to_all(left_rows, 'px', 2, 1, tiled=True)  272 us
    all_gather x1, waiting for transfers between devices, outgoing_sum(): right_cols = lax.all_gather(right_op, 'px', axis=1, tiled=True)  110 us
    dot_general x2, local copies, waits for them, and re-layouts, gated_operands(): jnp.einsum('ijd,de->eij', normed, w_in[:, :proj_width], preferred_element...  72.3 us
    all_to_all x2, local copies, waits for them, and re-layouts, incoming_sum(): left_cols = lax.all_to_all(left_rows, 'px', 2, 1, tiled=True)  60.9 us
    all_to_all x2, local copies, waits for them, and re-layouts, outgoing_sum(): right_rows = lax.all_to_all(right_cols, 'py', 1, 2, tiled=True)  47 us
    add x2, other arithmetic, gated_operands(): projected = projected + b_in[:proj_width].astype(jnp.float32)[:, None, None]  46.1 us
  transfers between devices with their start and end apart: 5, of which 3 were waited for; matrix products, arithmetic and copies ran while one was open for 4% of the time, Pallas kernels for 0%

commit v1 on v0

v1 whole, which is shorter than its diff:
```python
import functools

import jax
import jax.numpy as jnp
from jax import lax
from jax.experimental import pallas as pl
from jax.experimental.pallas import tpu as pltpu
from jax.sharding import PartitionSpec as P

LN_EPS = 1e-5
MESH = pl.DeviceIdType.MESH
F32, BF16 = jnp.float32, jnp.bfloat16
ROWS = 16
TO_RIGHT, TO_LEFT, TO_PARTNER, TO_MIRROR = 0, 1, 2, 3


def norm_major(values, gain, shift):
    average = jnp.mean(values, axis=0, keepdims=True)
    centered = values - average
    variance = jnp.mean(centered * centered, axis=0, keepdims=True)
    return centered * lax.rsqrt(variance + LN_EPS) * gain + shift


def remote(src, dst, send_sem, recv_sem, device):
    return pltpu.make_async_remote_copy(src_ref=src, dst_ref=dst, send_sem=send_sem, recv_sem=recv_sem, device_id=device, device_id_type=MESH)


def landed(ref, sem):
    pltpu.make_async_copy(ref, ref, sem).wait()


def project(rows, mask, w_ref, b_ref, base, stage, dst, at):
    w = w_ref[base:base + 256, :]
    for r in range(0, ROWS, 2):
        pair = jnp.concatenate([rows(r), rows(r + 1)], axis=1)
        prod = jnp.dot(w, pair, preferred_element_type=F32)
        for t in range(2):
            gate = prod[:128, 128 * t:128 * t + 128] + b_ref[base:base + 128, :]
            value = prod[128:, 128 * t:128 * t + 128] + b_ref[base + 128:base + 256, :]
            stage[r + t] = mask[r + t:r + t + 1] * jax.nn.sigmoid(gate) * value
    dst[:, pl.ds(at, ROWS), :] = jnp.transpose(stage[...], (1, 0, 2)).astype(BF16)


def finish_rows(n, x_ref, z_row, zn_row, w_ref, b_ref, wo_ref, bo_ref, lo_ref, stage, emit):
    i0 = pl.multiple_of(n * 8, 8)
    x = x_ref[:, pl.ds(i0, 8), :]
    average = jnp.mean(x, axis=0)
    centered = x - average[None]
    variance = jnp.mean(centered * centered, axis=0)
    scale = lax.rsqrt(variance + LN_EPS)
    stage[...] = jnp.transpose(centered * scale[None], (1, 0, 2))
    for r in range(0, 8, 2):
        pair = [(stage[r + t] * lo_ref[0] + lo_ref[1]).astype(BF16) for t in range(2)]
        update = jnp.dot(wo_ref[...], jnp.concatenate(pair, axis=1), preferred_element_type=F32)
        zn = jnp.concatenate([zn_row(i0 + r), zn_row(i0 + r + 1)], axis=1)
        gate = jnp.dot(w_ref[512:640, :], zn, preferred_element_type=F32)
        for t in range(2):
            lanes = slice(128 * t, 128 * t + 128)
            g = jax.nn.sigmoid(gate[:, lanes] + b_ref[512:640, :])
            emit(i0 + r + t, z_row(i0 + r + t).astype(F32) + g * (update[:, lanes] + bo_ref[...]))


def near_order(q, s):
    first = q + 1 - 2 * lax.rem(q, 2)
    second = 2 - lax.div(q, 2)
    third = 3 - 3 * lax.div(q, 2)
    is0, is1, is2, is3 = (jnp.int32(1) * (s == v) for v in range(4))
    return is0 * q + is1 * first + is2 * second + is3 * third


def greet(p, q, everyone):
    barrier = pltpu.get_barrier_semaphore()
    peers = [lax.rem(p + d, 4) for d in (1, 2, 3)] if everyone else [p + 1 - 2 * lax.rem(p, 2), lax.rem(p + 2, 4)]
    for peer in peers:
        pl.semaphore_signal(barrier, inc=1, device_id={'px': peer}, device_id_type=MESH)

    @pl.when(q < 3)
    def _():
        pl.semaphore_signal(barrier, inc=1, device_id={'py': q + 1}, device_id_type=MESH)

    @pl.when(q > 0)
    def _():
        pl.semaphore_signal(barrier, inc=1, device_id={'py': q - 1}, device_id_type=MESH)

    edge = jnp.int32(1) * (q == 0) + jnp.int32(1) * (q == 3)
    pl.semaphore_wait(barrier, len(peers) + 2 - edge)


def outgoing_kernel(z_ref, mask_ref, w_ref, b_ref, li_ref, wo_ref, bo_ref, lo_ref, out_ref,
                    zb, mb, a_ref, bb_ref, x_ref, stage, stage8, ra, rb, rma, rmb, ss, sm):
    chunks = 128 // ROWS
    p, q = lax.axis_index('px'), lax.axis_index('py')
    partner, mirror = p + 1 - 2 * lax.rem(p, 2), lax.rem(p + 2, 4)
    right, left = {'py': q + 1}, {'py': q - 1}
    diag = p == q
    relay = p == lax.rem(q + 2, 4)
    bsel = 1 - jnp.int32(1) * diag

    greet(p, q, False)

    def rows_of(h):
        return pl.ds(pl.multiple_of(h * ROWS, ROWS), ROWS)

    def along(k, h, kind, dev):
        part = zb.at[0, k, rows_of(h)]
        remote(part, part, ss.at[kind, k], ra.at[k, h], dev).start()

    def across(which, k, h, kind, dev):
        remote(zb.at[which, k, rows_of(h)], zb.at[1, k, rows_of(h)], ss.at[kind, k], rb.at[k, h], dev).start()

    def along_mask(k, kind, dev):
        remote(mb.at[0, k], mb.at[0, k], sm.at[kind, k], rma.at[k], dev).start()

    def across_mask(which, k, kind, dev):
        remote(mb.at[which, k], mb.at[1, k], sm.at[kind, k], rmb.at[k], dev).start()

    def spread(k, h, first):
        @pl.when(jnp.logical_and(q < 3, k <= q))
        def _():
            along(k, h, TO_RIGHT, right)
            if first is not None:
                pl.when(first)(lambda: along_mask(k, TO_RIGHT, right))

        @pl.when(jnp.logical_and(q > 0, k >= q))
        def _():
            along(k, h, TO_LEFT, left)
            if first is not None:
                pl.when(first)(lambda: along_mask(k, TO_LEFT, left))

        @pl.when(diag)
        def _():
            across(0, k, h, TO_MIRROR, {'px': mirror})
            across(0, k, h, TO_PARTNER, {'px': partner})
            if first is not None:
                @pl.when(first)
                def _():
                    across_mask(0, k, TO_MIRROR, {'px': mirror})
                    across_mask(0, k, TO_PARTNER, {'px': partner})

    mb[0, q] = mask_ref[...]

    @pl.loop(0, chunks)
    def _(h):
        for r in range(ROWS):
            i = h * ROWS + r
            zt = jnp.transpose(z_ref[i].astype(F32))
            out_ref[i] = zt.astype(BF16)
            zb[0, q, i] = norm_major(zt, li_ref[0], li_ref[1]).astype(BF16)

        @pl.when(h > 0)
        def _():
            spread(q, h - 1, h == 1)

    @pl.loop(0, 128)
    def _(c):
        x_ref[c] = jnp.zeros((128, 128), F32)

    spread(q, jnp.int32(chunks - 1), None)

    @pl.loop(0, 4)
    def _(s):
        k = near_order(q, s)

        @pl.loop(0, chunks)
        def _(h):
            @pl.when(s > 0)
            def _():
                landed(zb.at[0, k, rows_of(h)], ra.at[k, h])
                pl.when(h == 0)(lambda: landed(mb.at[0, k], rma.at[k]))
                spread(k, h, h == 0)

            @pl.when(jnp.logical_not(diag))
            def _():
                landed(zb.at[1, k, rows_of(h)], rb.at[k, h])
                pl.when(h == 0)(lambda: landed(mb.at[1, k], rmb.at[k]))

                @pl.when(relay)
                def _():
                    across(1, k, h, TO_PARTNER, {'px': partner})
                    pl.when(h == 0)(lambda: across_mask(1, k, TO_PARTNER, {'px': partner}))

            r0 = pl.multiple_of(h * ROWS, ROWS)
            mask_a = mb[0, k, pl.ds(r0, ROWS), :].astype(F32)
            project(lambda r: zb[0, k, r0 + r], mask_a, w_ref, b_ref, 0, stage, a_ref, r0)
            mask_b = mb[bsel, k, pl.ds(r0, ROWS), :].astype(F32)
            project(lambda r: zb[bsel, k, r0 + r], mask_b, w_ref, b_ref, 256, stage, bb_ref, r0)

        @pl.loop(0, 128 // 16)
        def _(n):
            for u in range(16):
                c = n * 16 + u
                x_ref[c] += lax.dot_general(a_ref[c], bb_ref[c], (((1,), (1,)), ((), ())), preferred_element_type=F32)

    @pl.loop(0, 16)
    def _(n):
        def emit(i, value):
            out_ref[i] = value.astype(BF16)
        finish_rows(n, x_ref, lambda i: out_ref[i], lambda i: zb[0, q, i], w_ref, b_ref, wo_ref, bo_ref, lo_ref, stage8, emit)

    for k in range(4):
        def drain(kind, when):
            @pl.when(when)
            def _():
                landed(zb.at[0, k], ss.at[kind, k])
                landed(mb.at[0, k], sm.at[kind, k])
        drain(TO_RIGHT, jnp.logical_and(q < 3, k <= q))
        drain(TO_LEFT, jnp.logical_and(q > 0, k >= q))
        drain(TO_MIRROR, diag)
        drain(TO_PARTNER, jnp.logical_or(diag, relay))


VM = pl.BlockSpec(memory_space=pltpu.VMEM)
ANY = pl.BlockSpec(memory_space=pl.ANY)
DMA = pltpu.SemaphoreType.DMA


def outgoing(z, mask, wt, bias, ln_in, wo, bo, ln_out):
    return pl.pallas_call(
        outgoing_kernel,
        out_shape=jax.ShapeDtypeStruct((128, 128, 128), BF16),
        in_specs=[VM] * 8,
        out_specs=VM,
        scratch_shapes=[
            pltpu.VMEM((2, 4, 128, 128, 128), BF16),
            pltpu.VMEM((2, 4, 128, 128), BF16),
            pltpu.VMEM((128, 128, 128), BF16),
            pltpu.VMEM((128, 128, 128), BF16),
            pltpu.VMEM((128, 128, 128), F32),
            pltpu.VMEM((ROWS, 128, 128), F32),
            pltpu.VMEM((8, 128, 128), F32),
            DMA((4, 128 // ROWS)), DMA((4, 128 // ROWS)), DMA((4,)), DMA((4,)), DMA((4, 4)), DMA((4, 4)),
        ],
        compiler_params=pltpu.CompilerParams(collective_id=0, has_side_effects=True, vmem_limit_bytes=67043328),
        name='outgoing',
    )(z, mask, wt, bias, ln_in, wo, bo, ln_out)


def incoming_kernel(z_ref, mask_ref, w_ref, b_ref, li_ref, wo_ref, bo_ref, lo_ref, out_ref, col,
                    zz, mm, mc, a_ref, bb_ref, x_ref, stage, stage8, rc, ra, rb, lc, rmc, rma, rmb, io, ss, sm, sp, spm):
    chunks = 128 // ROWS
    p, q = lax.axis_index('px'), lax.axis_index('py')
    partner, mirror = p + 1 - 2 * lax.rem(p, 2), lax.rem(p + 2, 4)
    right, left = {'py': q + 1}, {'py': q - 1}
    diag = p == q
    off_diag = jnp.logical_not(diag)
    asel = jnp.int32(1) * diag

    greet(p, q, True)
    load = pltpu.make_async_copy(z_ref, a_ref.at[:, 0:128, :], io.at[0])
    load.start()

    def rows_of(h):
        return pl.ds(pl.multiple_of(h * ROWS, ROWS), ROWS)

    def to_line(src, m, h, kind, dev):
        remote(src, col.at[m, rows_of(h)], ss.at[kind, m], rc.at[m, h], dev).start()

    def to_line_mask(src, m, kind, dev):
        remote(src, mc.at[m], sm.at[kind, m], rmc.at[m], dev).start()

    def plane(src, which, k, h, sem, rsem, dev):
        remote(src, zz.at[which, k, rows_of(h)], sem, rsem, dev).start()

    def own(h, first):
        part = zz.at[1, p, rows_of(h)]

        @pl.when(q < 3)
        def _():
            to_line(part, q, h, TO_RIGHT, right)
            if first is not None:
                pl.when(first)(lambda: to_line_mask(mm.at[1, p], q, TO_RIGHT, right))

        @pl.when(q > 0)
        def _():
            to_line(part, q, h, TO_LEFT, left)
            if first is not None:
                pl.when(first)(lambda: to_line_mask(mm.at[1, p], q, TO_LEFT, left))
        plane(part, 1, p, h, sp.at[0], rb.at[p, h], {'px': mirror})
        plane(part, 1, p, h, sp.at[1], rb.at[p, h], {'px': partner})
        if first is not None:
            @pl.when(first)
            def _():
                remote(mm.at[1, p], mm.at[1, p], spm.at[0], rmb.at[p], {'px': mirror}).start()
                remote(mm.at[1, p], mm.at[1, p], spm.at[1], rmb.at[p], {'px': partner}).start()

    mm[1, p] = mask_ref[...]
    load.wait()

    @pl.loop(0, chunks)
    def _(h):
        for r in range(ROWS):
            i = h * ROWS + r
            zt = a_ref[i, 0:128, :].astype(F32)
            zz[1, p, i] = norm_major(zt, li_ref[0], li_ref[1]).astype(BF16)

        @pl.when(h > 0)
        def _():
            own(h - 1, h == 1)

    @pl.loop(0, 128)
    def _(c):
        x_ref[c] = jnp.zeros((128, 128), F32)

    own(jnp.int32(chunks - 1), None)

    def pass_on(s, m, h):
        landed(col.at[m, rows_of(h)], rc.at[m, h])
        pl.when(h == 0)(lambda: landed(mc.at[m], rmc.at[m]))
        part = col.at[m, rows_of(h)]

        @pl.when(jnp.logical_and(q < 3, m < q))
        def _():
            to_line(part, m, h, TO_RIGHT, right)
            pl.when(h == 0)(lambda: to_line_mask(mc.at[m], m, TO_RIGHT, right))

        @pl.when(jnp.logical_and(q > 0, m > q))
        def _():
            to_line(part, m, h, TO_LEFT, left)
            pl.when(h == 0)(lambda: to_line_mask(mc.at[m], m, TO_LEFT, left))

        @pl.when(m != p)
        def _():
            plane(part, 0, p, h, ss.at[2, m], ra.at[p, h], {'px': m})
            pl.when(h == 0)(lambda: remote(mc.at[m], mm.at[0, p], sm.at[2, m], rma.at[p], {'px': m}).start())

        @pl.when(m == p)
        def _():
            pltpu.make_async_copy(part, zz.at[0, p, rows_of(h)], lc.at[h]).start()

            @pl.when(h == 0)
            def _():
                mm[0, p] = mc[p]

        @pl.when(s == 1)
        def _():
            landed(zz.at[1, mirror, rows_of(h)], rb.at[mirror, h])
            plane(zz.at[1, mirror, rows_of(h)], 1, mirror, h, sp.at[2], rb.at[mirror, h], {'px': partner})

            @pl.when(h == 0)
            def _():
                landed(mm.at[1, mirror], rmb.at[mirror])
                remote(mm.at[1, mirror], mm.at[1, mirror], spm.at[2], rmb.at[mirror], {'px': partner}).start()

    def compute(h):
        r0 = pl.multiple_of(h * ROWS, ROWS)

        @pl.loop(0, 4)
        def _(k):
            @pl.when(jnp.logical_and(k != p, k != mirror))
            def _():
                landed(zz.at[1, k, rows_of(h)], rb.at[k, h])
                pl.when(h == 0)(lambda: landed(mm.at[1, k], rmb.at[k]))

            @pl.when(jnp.logical_and(off_diag, k != p))
            def _():
                landed(zz.at[0, k, rows_of(h)], ra.at[k, h])
                pl.when(h == 0)(lambda: landed(mm.at[0, k], rma.at[k]))

            @pl.when(jnp.logical_and(off_diag, k == p))
            def _():
                landed(zz.at[0, k, rows_of(h)], lc.at[h])

            at = pl.multiple_of(k * 64 + lax.rem(h, 4) * ROWS, ROWS)
            mask_b = mm[1, k, pl.ds(r0, ROWS), :].astype(F32)
            project(lambda r: zz[1, k, r0 + r], mask_b, w_ref, b_ref, 256, stage, bb_ref, at)
            mask_a = mm[asel, k, pl.ds(r0, ROWS), :].astype(F32)
            project(lambda r: zz[asel, k, r0 + r], mask_a, w_ref, b_ref, 0, stage, a_ref, at)

        @pl.when(lax.rem(h, 4) == 3)
        def _():
            @pl.loop(0, 128 // 8)
            def _(n):
                for u in range(8):
                    c = n * 8 + u
                    x_ref[c] += lax.dot_general(a_ref[c], bb_ref[c], (((0,), (0,)), ((), ())), preferred_element_type=F32)

    @pl.loop(1, 4)
    def _(s):
        m = near_order(q, s)
        mine = jnp.logical_or(m == p, jnp.logical_and(diag, s == 1))

        @pl.loop(0, chunks + 1)
        def _(h):
            @pl.when(h < chunks)
            def _():
                pass_on(s, m, h)

            @pl.when(jnp.logical_and(h > 0, mine))
            def _():
                compute(h - 1)

    load.start()
    load.wait()

    def store(n):
        rows = pl.ds(pl.multiple_of(n * 8, 8), 8)
        return pltpu.make_async_copy(bb_ref.at[rows, 0:128, :], out_ref.at[rows], io.at[1])

    @pl.loop(0, 16)
    def _(n):
        def emit(i, value):
            bb_ref[i, 0:128, :] = jnp.transpose(value).astype(BF16)
        finish_rows(n, x_ref, lambda i: a_ref[i, 0:128, :], lambda i: zz[1, p, i], w_ref, b_ref, wo_ref, bo_ref, lo_ref, stage8, emit)
        pl.when(n > 0)(lambda: store(n - 1).start())

    store(jnp.int32(15)).start()

    for m in range(4):
        def drain(kind, when):
            @pl.when(when)
            def _():
                landed(col.at[m], ss.at[kind, m])
                landed(mc.at[m], sm.at[kind, m])
        drain(TO_RIGHT, jnp.logical_and(q < 3, m <= q))
        drain(TO_LEFT, jnp.logical_and(q > 0, m >= q))
        drain(2, jnp.logical_and(m != q, m != p))
    for kind in range(3):
        landed(zz.at[1, 0], sp.at[kind])
        landed(mm.at[1, 0], spm.at[kind])
    pltpu.make_async_copy(bb_ref.at[:, 0:128, :], out_ref, io.at[1]).wait()


def incoming(z, mask, wt, bias, ln_in, wo, bo, ln_out):
    n = 128 // ROWS
    return pl.pallas_call(
        incoming_kernel,
        out_shape=[jax.ShapeDtypeStruct((128, 128, 128), BF16), jax.ShapeDtypeStruct((4, 128, 128, 128), BF16)],
        in_specs=[ANY] + [VM] * 7,
        out_specs=[ANY, ANY],
        scratch_shapes=[
            pltpu.VMEM((2, 4, 128, 128, 128), BF16),
            pltpu.VMEM((2, 4, 128, 128), BF16),
            pltpu.VMEM((4, 128, 128), BF16),
            pltpu.VMEM((128, 256, 128), BF16),
            pltpu.VMEM((128, 256, 128), BF16),
            pltpu.VMEM((128, 128, 128), F32),
            pltpu.VMEM((ROWS, 128, 128), F32),
            pltpu.VMEM((8, 128, 128), F32),
            DMA((4, n)), DMA((4, n)), DMA((4, n)), DMA((n,)), DMA((4,)), DMA((4,)), DMA((4,)), DMA((2,)),
            DMA((3, 4)), DMA((3, 4)), DMA((3,)), DMA((3,)),
        ],
        compiler_params=pltpu.CompilerParams(collective_id=1, has_side_effects=True, vmem_limit_bytes=67043328),
        name='incoming',
    )(z, mask, wt, bias, ln_in, wo, bo, ln_out)[0]


def solution(mesh):
    pair_spec = P(('batch', 'px'), 'py', None)
    mask_spec = P(('batch', 'px'), 'py')
    whole = P()

    def device_body(pair_blk, mask_blk, ln_in, w_in, b_in, ln_out, w_out, b_out):
        mask = mask_blk.astype(BF16)
        wt = jnp.swapaxes(w_in, 1, 2)
        wo = jnp.swapaxes(w_out, 1, 2)
        def wide(v):
            return jnp.broadcast_to(v.astype(F32)[..., None], v.shape + (128,))
        bias, bo, li, lo = wide(b_in), wide(b_out), wide(ln_in), wide(ln_out)
        z1 = outgoing(pair_blk, mask, wt[0], bias[0], li[0], wo[0], bo[0], lo[0])
        return incoming(z1, mask, wt[1], bias[1], li[1], wo[1], bo[1], lo[1])

    return jax.shard_map(device_body, mesh=mesh, in_specs=(pair_spec, mask_spec, whole, whole, whole, whole, whole, whole), out_specs=pair_spec, check_vma=False)
```

time: 1750 us -> 739 us (0.42)
  waiting for transfers between devices: 1020 us -> 0 us
  Pallas kernels: 0 us -> 720 us
  blocking collectives: 272 us -> 0 us
  local copies, waits for them, and re-layouts: 234 us -> 14.5 us
  other arithmetic: 101 us -> 4.15 us
  matrix products: 79.5 us -> 0 us
    pallas_call x0 -> x2, Pallas kernels: none -> 720 us  [the longest x1 407 us: incoming(): pl.pallas_call(incoming_kernel, out_shape=[jax.ShapeDtypeStruct((128, 128...]
    all_to_all x1 -> x0, waiting for transfers between devices: 629 us -> none  [outgoing_sum(): right_rows = lax.all_to_all(right_cols, 'py', 1, 2, tiled=True)]
    all_gather x4 -> x0, waiting for transfers between devices: 395 us -> none  [the longest x1 284 us: incoming_sum(): left_rows = lax.all_gather(left_op, 'py', axis=2, tiled=True)]
    all_to_all x1 -> x0, blocking collectives: 272 us -> none  [incoming_sum(): left_cols = lax.all_to_all(left_rows, 'px', 2, 1, tiled=True)]
    all_to_all x4 -> x0, local copies, waits for them, and re-layouts: 108 us -> none  [the longest x2 60.9 us: incoming_sum(): left_cols = lax.all_to_all(left_rows, 'px', 2, 1, tiled=True)]
    dot_general x8 -> x0, matrix products: 79.5 us -> none  [the longest x2 29.2 us: gated_operands(): jnp.einsum('ijd,de->eij', normed, w_in[:, :proj_width], preferred_element...]
    dot_general x2 -> x0, local copies, waits for them, and re-layouts: 72.3 us -> none  [gated_operands(): jnp.einsum('ijd,de->eij', normed, w_in[:, :proj_width], preferred_element...]
    add x2 -> x0, other arithmetic: 46.1 us -> none  [gated_operands(): projected = projected + b_in[:proj_width].astype(jnp.float32)[:, None, None]]
  transfers between devices with their start and end apart: 5 -> 0, of which waited for: 3 -> 0; matrix products, arithmetic and copies ran while one was open for 4% -> 0% of each run, Pallas kernels for 0% -> 0%
where the time goes in v1:
time: 739 us; the launch traced here: 738 us
  Pallas kernels  720 us (97%)
  local copies, waits for them, and re-layouts  14.5 us (2%)
    pallas_call x1, Pallas kernels, incoming(): pl.pallas_call(incoming_kernel, out_shape=[jax.ShapeDtypeStruct((128, 128...  407 us
    pallas_call x1, Pallas kernels, outgoing(): pl.pallas_call(outgoing_kernel, out_shape=jax.ShapeDtypeStruct((128, 128,...  313 us

profile of v1, /device:TPU:26, one launch (start us, length us, event | category | flops | bytes accessed | tf_op | source)
XLA Modules:
  0.0 738.2 jit_solution(15155831600592492780)
XLA Ops:
  0.0 0.7 convert_element_type.18
  0.7 0.7 convert_element_type.17
  1.4 0.7 convert_element_type.19
  2.0 0.7 convert_element_type.16
  2.7 1.4 convert_element_type.15.mask_ref
  4.2 0.7 broadcast_in_dim.61.bo_ref
  4.9 0.7 broadcast_in_dim.53.bo_ref
  5.6 0.9 copy.10
  6.6 0.6 slice_bitcast_fusion.2
  7.2 0.8 broadcast_in_dim.63.lo_ref
  7.9 0.8 broadcast_in_dim.59.li_ref
  8.7 0.7 broadcast_in_dim.55.lo_ref
  9.4 0.7 broadcast_in_dim.51.li_ref
  10.2 0.9 broadcast_in_dim.57.b_ref
  11.1 0.9 broadcast_in_dim.49.b_ref
  12.0 1.2 copy.9
  13.1 0.7 slice_bitcast_fusion
  13.9 312.8 %outgoing.1.z_ref = bf16[128,128,128]{2,1,0:T(8,128)(2,1)} custom-call(bf16[128,128,128]{2,1,0:T(8,128)(2,1)} %z_ref.1, bf16[128,128]{1,0:T(8,128)(2,1)} %convert_element_type.15.mask_ref, bf16[640,128]{1,0:T(8,128)(2,1)} %get-tuple-element.10.w_ref, f32[640,128]{1,0:T(8,128)} %broadcast_in_dim.49.b_ref, f32[2,128,128]{2,1,0:T(8,128)} %broadcast_in_dim.51.li_ref, ...), custom_call_target="tpu_custom_call" | custom-call | tf_op jit(solution)/shard_map/outgoing/pallas_call | solution.py:218
  326.7 406.7 %incoming.1 = (bf16[128,128,128]{2,1,0:T(8,128)(2,1)}, bf16[4,128,128,128]{3,2,1,0:T(8,128)(2,1)}) custom-call(bf16[128,128,128]{2,1,0:T(8,128)(2,1)} %outgoing.1.z_ref, bf16[128,128]{1,0:T(8,128)(2,1)} %convert_element_type.15.mask_ref, bf16[640,128]{1,0:T(8,128)(2,1)} %get-tuple-element.9.w_ref, f32[640,128]{1,0:T(8,128)} %broadcast_in_dim.57.b_ref, ...), custom_call_target="tpu_custom_call" | custom-call | tf_op jit(solution)/shard_map/incoming/pallas_call | solution.py:425
  733.4 4.8 copy.12
  (4 shorter events, 0.0 us)

commit v2 on v1

--- a/solution.py
+++ b/solution.py
@@ -374,20 +374,26 @@
                     c = n * 8 + u
                     x_ref[c] += lax.dot_general(a_ref[c], bb_ref[c], (((0,), (0,)), ((), ())), preferred_element_type=F32)
 
+    third = 3 - 3 * lax.div(q, 2)
+    second = 2 - lax.div(q, 2)
+    last = p == third
+    slot = jnp.where(p == second, 3, 2)
+
     @pl.loop(1, 4)
     def _(s):
         m = near_order(q, s)
-        mine = jnp.logical_or(m == p, jnp.logical_and(diag, s == 1))
-
-        @pl.loop(0, chunks + 1)
+        lag = jnp.where(last, 2, 0)
+        when = jnp.where(last, 3, slot)
+
+        @pl.loop(0, chunks + 2 * lax.div(s, 3))
         def _(h):
             @pl.when(h < chunks)
             def _():
                 pass_on(s, m, h)
 
-            @pl.when(jnp.logical_and(h > 0, mine))
-            def _():
-                compute(h - 1)
+            @pl.when(jnp.logical_and(s == when, jnp.logical_and(h >= lag, h < chunks + lag)))
+            def _():
+                compute(h - lag)
 
     load.start()
     load.wait()

time: 739 us -> 651 us (0.88)
  Pallas kernels: 720 us -> 632 us
    pallas_call x1, Pallas kernels: 407 us -> 319 us  [incoming(): pl.pallas_call(incoming_kernel, out_shape=[jax.ShapeDtypeStruct((128, 128...]
where the time goes in v2:
time: 651 us; the launch traced here: 650 us
  Pallas kernels  632 us (97%)
  local copies, waits for them, and re-layouts  14.5 us (2%)
    pallas_call x1, Pallas kernels, incoming(): pl.pallas_call(incoming_kernel, out_shape=[jax.ShapeDtypeStruct((128, 128...  319 us
    pallas_call x1, Pallas kernels, outgoing(): pl.pallas_call(outgoing_kernel, out_shape=jax.ShapeDtypeStruct((128, 128,...  313 us

profile of v2, /device:TPU:26, one launch (start us, length us, event | category | flops | bytes accessed | tf_op | source)
XLA Modules:
  0.0 650.3 jit_solution(18004447322210572638)
XLA Ops:
  0.0 0.7 convert_element_type.18
  0.7 0.7 convert_element_type.17
  1.4 0.7 convert_element_type.19
  2.0 0.7 convert_element_type.16
  2.7 1.4 convert_element_type.15.mask_ref
  4.2 0.7 broadcast_in_dim.61.bo_ref
  4.9 0.7 broadcast_in_dim.53.bo_ref
  5.6 0.9 copy.10
  6.6 0.6 slice_bitcast_fusion.2
  7.2 0.8 broadcast_in_dim.63.lo_ref
  7.9 0.8 broadcast_in_dim.59.li_ref
  8.7 0.7 broadcast_in_dim.55.lo_ref
  9.4 0.7 broadcast_in_dim.51.li_ref
  10.2 0.9 broadcast_in_dim.57.b_ref
  11.1 0.9 broadcast_in_dim.49.b_ref
  12.0 1.2 copy.9
  13.1 0.7 slice_bitcast_fusion
  13.9 312.8 %outgoing.1.z_ref = bf16[128,128,128]{2,1,0:T(8,128)(2,1)} custom-call(bf16[128,128,128]{2,1,0:T(8,128)(2,1)} %z_ref.1, bf16[128,128]{1,0:T(8,128)(2,1)} %convert_element_type.15.mask_ref, bf16[640,128]{1,0:T(8,128)(2,1)} %get-tuple-element.10.w_ref, f32[640,128]{1,0:T(8,128)} %broadcast_in_dim.49.b_ref, f32[2,128,128]{2,1,0:T(8,128)} %broadcast_in_dim.51.li_ref, ...), custom_call_target="tpu_custom_call" | custom-call | tf_op jit(solution)/shard_map/outgoing/pallas_call | solution.py:218
  326.7 318.8 %incoming.1 = (bf16[128,128,128]{2,1,0:T(8,128)(2,1)}, bf16[4,128,128,128]{3,2,1,0:T(8,128)(2,1)}) custom-call(bf16[128,128,128]{2,1,0:T(8,128)(2,1)} %outgoing.1.z_ref, bf16[128,128]{1,0:T(8,128)(2,1)} %convert_element_type.15.mask_ref, bf16[640,128]{1,0:T(8,128)(2,1)} %get-tuple-element.9.w_ref, f32[640,128]{1,0:T(8,128)} %broadcast_in_dim.57.b_ref, ...), custom_call_target="tpu_custom_call" | custom-call | tf_op jit(solution)/shard_map/incoming/pallas_call | solution.py:431
  645.5 4.8 copy.12
  (4 shorter events, 0.0 us)

commit v3 on v2

--- a/solution.py
+++ b/solution.py
@@ -60,9 +60,11 @@
             emit(i0 + r + t, z_row(i0 + r + t).astype(F32) + g * (update[:, lanes] + bo_ref[...]))
 
 
-def near_order(q, s):
-    first = q + 1 - 2 * lax.rem(q, 2)
-    second = 2 - lax.div(q, 2)
+def near_order(q, s, update):
+    if update == 0:
+        first, second = q + 1 - 2 * lax.rem(q, 2), 2 - lax.div(q, 2)
+    else:
+        first, second = 2 - lax.div(q, 2), q + 1 - 2 * lax.rem(q, 2)
     third = 3 - 3 * lax.div(q, 2)
     is0, is1, is2, is3 = (jnp.int32(1) * (s == v) for v in range(4))
     return is0 * q + is1 * first + is2 * second + is3 * third
@@ -86,33 +88,42 @@
     pl.semaphore_wait(barrier, len(peers) + 2 - edge)
 
 
-def outgoing_kernel(z_ref, mask_ref, w_ref, b_ref, li_ref, wo_ref, bo_ref, lo_ref, out_ref,
-                    zb, mb, a_ref, bb_ref, x_ref, stage, stage8, ra, rb, rma, rmb, ss, sm):
+def kernel(z_ref, mask_ref, li_in, w_in, b_in, lo_in, wo_in, bo_in, out_ref, col, keep,
+           w_refs, b_refs, li_refs, wo_refs, bo_refs, lo_refs, zz, mb, mm, mc, a_ref, bb_ref, x_ref, stage, stage8,
+           ra1, rb1, rma1, rmb1, ss1, sm1, rc, ra, rb, lc, rmc, rma, rmb, io, ss, sm, sp, spm, free):
     chunks = 128 // ROWS
     p, q = lax.axis_index('px'), lax.axis_index('py')
     partner, mirror = p + 1 - 2 * lax.rem(p, 2), lax.rem(p + 2, 4)
     right, left = {'py': q + 1}, {'py': q - 1}
     diag = p == q
+    off_diag = jnp.logical_not(diag)
     relay = p == lax.rem(q + 2, 4)
-    bsel = 1 - jnp.int32(1) * diag
-
-    greet(p, q, False)
+    asel = jnp.int32(1) * diag
+    bsel = 1 - asel
+    plane_peers = [lax.rem(p + d, 4) for d in (1, 2, 3)]
+
+    greet(p, q, True)
+    load = pltpu.make_async_copy(z_ref, bb_ref.at[:, 128:256, :], io.at[0])
+    load.start()
 
     def rows_of(h):
         return pl.ds(pl.multiple_of(h * ROWS, ROWS), ROWS)
 
+    w_ref, b_ref, li_ref, wo_ref, bo_ref, lo_ref = (r.at[0] for r in (w_refs, b_refs, li_refs, wo_refs, bo_refs, lo_refs))
+    zb = zz
+
     def along(k, h, kind, dev):
         part = zb.at[0, k, rows_of(h)]
-        remote(part, part, ss.at[kind, k], ra.at[k, h], dev).start()
+        remote(part, part, ss1.at[kind, k], ra1.at[k, h], dev).start()
 
     def across(which, k, h, kind, dev):
-        remote(zb.at[which, k, rows_of(h)], zb.at[1, k, rows_of(h)], ss.at[kind, k], rb.at[k, h], dev).start()
+        remote(zb.at[which, k, rows_of(h)], zb.at[1, k, rows_of(h)], ss1.at[kind, k], rb1.at[k, h], dev).start()
 
     def along_mask(k, kind, dev):
-        remote(mb.at[0, k], mb.at[0, k], sm.at[kind, k], rma.at[k], dev).start()
+        remote(mb.at[0, k], mb.at[0, k], sm1.at[kind, k], rma1.at[k], dev).start()
 
     def across_mask(which, k, kind, dev):
-        remote(mb.at[which, k], mb.at[1, k], sm.at[kind, k], rmb.at[k], dev).start()
+        remote(mb.at[which, k], mb.at[1, k], sm1.at[kind, k], rmb1.at[k], dev).start()
 
     def spread(k, h, first):
         @pl.when(jnp.logical_and(q < 3, k <= q))
@@ -137,14 +148,25 @@
                     across_mask(0, k, TO_MIRROR, {'px': mirror})
                     across_mask(0, k, TO_PARTNER, {'px': partner})
 
-    mb[0, q] = mask_ref[...]
+    mask = mask_ref[...].astype(F32).astype(BF16)
+    mb[0, q] = mask
+    mm[1, p] = mask
+
+    def wide(row):
+        return jnp.transpose(jnp.broadcast_to(row.astype(F32), (128, 128)))
+
+    for u in range(2):
+        ln_rows = li_in[u].astype(F32)
+        for t in range(2):
+            li_refs[u, t] = wide(ln_rows[t:t + 1])
+    load.wait()
 
     @pl.loop(0, chunks)
     def _(h):
         for r in range(ROWS):
             i = h * ROWS + r
-            zt = jnp.transpose(z_ref[i].astype(F32))
-            out_ref[i] = zt.astype(BF16)
+            zt = jnp.transpose(bb_ref[i, 128:256, :].astype(F32))
+            a_ref[i, 128:256, :] = zt.astype(BF16)
             zb[0, q, i] = norm_major(zt, li_ref[0], li_ref[1]).astype(BF16)
 
         @pl.when(h > 0)
@@ -157,22 +179,33 @@
 
     spread(q, jnp.int32(chunks - 1), None)
 
+    b_rows, bo_rows = b_in[...].astype(F32), bo_in[...].astype(F32)
+    for u in range(2):
+        lo_rows = lo_in[u].astype(F32)
+        for t in range(2):
+            lo_refs[u, t] = wide(lo_rows[t:t + 1])
+        bo_refs[u] = wide(bo_rows[u:u + 1])
+        wo_refs[u] = jnp.transpose(wo_in[u].astype(F32)).astype(BF16)
+        for e in range(0, 640, 128):
+            b_refs[u, e:e + 128, :] = wide(b_rows[u:u + 1, e:e + 128])
+            w_refs[u, e:e + 128, :] = jnp.transpose(w_in[u, :, e:e + 128].astype(F32)).astype(BF16)
+
     @pl.loop(0, 4)
     def _(s):
-        k = near_order(q, s)
+        k = near_order(q, s, 0)
 
         @pl.loop(0, chunks)
         def _(h):
             @pl.when(s > 0)
             def _():
-                landed(zb.at[0, k, rows_of(h)], ra.at[k, h])
-                pl.when(h == 0)(lambda: landed(mb.at[0, k], rma.at[k]))
+                landed(zb.at[0, k, rows_of(h)], ra1.at[k, h])
+                pl.when(h == 0)(lambda: landed(mb.at[0, k], rma1.at[k]))
                 spread(k, h, h == 0)
 
             @pl.when(jnp.logical_not(diag))
             def _():
-                landed(zb.at[1, k, rows_of(h)], rb.at[k, h])
-                pl.when(h == 0)(lambda: landed(mb.at[1, k], rmb.at[k]))
+                landed(zb.at[1, k, rows_of(h)], rb1.at[k, h])
+                pl.when(h == 0)(lambda: landed(mb.at[1, k], rmb1.at[k]))
 
                 @pl.when(relay)
                 def _():
@@ -189,119 +222,82 @@
         def _(n):
             for u in range(16):
                 c = n * 16 + u
-                x_ref[c] += lax.dot_general(a_ref[c], bb_ref[c], (((1,), (1,)), ((), ())), preferred_element_type=F32)
+                x_ref[c] += lax.dot_general(a_ref[c, 0:128, :], bb_ref[c, 0:128, :], (((1,), (1,)), ((), ())), preferred_element_type=F32)
+
+    def to_line(src, m, h, kind, dev):
+        remote(src, col.at[m, rows_of(h)], ss.at[kind, m], rc.at[m, h], dev).start()
+
+    def to_line_mask(src, m, kind, dev):
+        remote(src, mc.at[m], sm.at[kind, m], rmc.at[m], dev).start()
+
+    def plane(src, which, k, h, sem, rsem, dev):
+        remote(src, zz.at[which, k, rows_of(h)], sem, rsem, dev).start()
+
+    def own_line(h, first):
+        part = zz.at[1, p, rows_of(h)]
+
+        @pl.when(jnp.logical_and(q < 3, q != 2))
+        def _():
+            to_line(part, q, h, TO_RIGHT, right)
+            pl.when(first)(lambda: to_line_mask(mm.at[1, p], q, TO_RIGHT, right))
+
+        @pl.when(jnp.logical_and(q > 0, q != 1))
+        def _():
+            to_line(part, q, h, TO_LEFT, left)
+            pl.when(first)(lambda: to_line_mask(mm.at[1, p], q, TO_LEFT, left))
+
+        @pl.when(first)
+        def _():
+            pl.semaphore_wait(free.at[0], 3)
+            remote(mm.at[1, p], mm.at[1, p], spm.at[0], rmb.at[p], {'px': mirror}).start()
+            remote(mm.at[1, p], mm.at[1, p], spm.at[1], rmb.at[p], {'px': partner}).start()
+        plane(part, 1, p, h, sp.at[0], rb.at[p, h], {'px': mirror})
+        plane(part, 1, p, h, sp.at[1], rb.at[p, h], {'px': partner})
+
+    @pl.when(relay)
+    def _():
+        for k in range(4):
+            landed(zz.at[1, k], ss1.at[TO_PARTNER, k])
+            landed(mb.at[1, k], sm1.at[TO_PARTNER, k])
+    for peer in plane_peers:
+        pl.semaphore_signal(free.at[0], inc=1, device_id={'px': peer}, device_id_type=MESH)
 
     @pl.loop(0, 16)
     def _(n):
         def emit(i, value):
-            out_ref[i] = value.astype(BF16)
-        finish_rows(n, x_ref, lambda i: out_ref[i], lambda i: zb[0, q, i], w_ref, b_ref, wo_ref, bo_ref, lo_ref, stage8, emit)
-
-    for k in range(4):
-        def drain(kind, when):
-            @pl.when(when)
-            def _():
-                landed(zb.at[0, k], ss.at[kind, k])
-                landed(mb.at[0, k], sm.at[kind, k])
-        drain(TO_RIGHT, jnp.logical_and(q < 3, k <= q))
-        drain(TO_LEFT, jnp.logical_and(q > 0, k >= q))
-        drain(TO_MIRROR, diag)
-        drain(TO_PARTNER, jnp.logical_or(diag, relay))
-
-
-VM = pl.BlockSpec(memory_space=pltpu.VMEM)
-ANY = pl.BlockSpec(memory_space=pl.ANY)
-DMA = pltpu.SemaphoreType.DMA
-
-
-def outgoing(z, mask, wt, bias, ln_in, wo, bo, ln_out):
-    return pl.pallas_call(
-        outgoing_kernel,
-        out_shape=jax.ShapeDtypeStruct((128, 128, 128), BF16),
-        in_specs=[VM] * 8,
-        out_specs=VM,
-        scratch_shapes=[
-            pltpu.VMEM((2, 4, 128, 128, 128), BF16),
-            pltpu.VMEM((2, 4, 128, 128), BF16),
-            pltpu.VMEM((128, 128, 128), BF16),
-            pltpu.VMEM((128, 128, 128), BF16),
-            pltpu.VMEM((128, 128, 128), F32),
-            pltpu.VMEM((ROWS, 128, 128), F32),
-            pltpu.VMEM((8, 128, 128), F32),
-            DMA((4, 128 // ROWS)), DMA((4, 128 // ROWS)), DMA((4,)), DMA((4,)), DMA((4, 4)), DMA((4, 4)),
-        ],
-        compiler_params=pltpu.CompilerParams(collective_id=0, has_side_effects=True, vmem_limit_bytes=67043328),
-        name='outgoing',
-    )(z, mask, wt, bias, ln_in, wo, bo, ln_out)
-
-
-def incoming_kernel(z_ref, mask_ref, w_ref, b_ref, li_ref, wo_ref, bo_ref, lo_ref, out_ref, col,
-                    zz, mm, mc, a_ref, bb_ref, x_ref, stage, stage8, rc, ra, rb, lc, rmc, rma, rmb, io, ss, sm, sp, spm):
-    chunks = 128 // ROWS
-    p, q = lax.axis_index('px'), lax.axis_index('py')
-    partner, mirror = p + 1 - 2 * lax.rem(p, 2), lax.rem(p + 2, 4)
-    right, left = {'py': q + 1}, {'py': q - 1}
-    diag = p == q
-    off_diag = jnp.logical_not(diag)
-    asel = jnp.int32(1) * diag
-
-    greet(p, q, True)
-    load = pltpu.make_async_copy(z_ref, a_ref.at[:, 0:128, :], io.at[0])
-    load.start()
-
-    def rows_of(h):
-        return pl.ds(pl.multiple_of(h * ROWS, ROWS), ROWS)
-
-    def to_line(src, m, h, kind, dev):
-        remote(src, col.at[m, rows_of(h)], ss.at[kind, m], rc.at[m, h], dev).start()
-
-    def to_line_mask(src, m, kind, dev):
-        remote(src, mc.at[m], sm.at[kind, m], rmc.at[m], dev).start()
-
-    def plane(src, which, k, h, sem, rsem, dev):
-        remote(src, zz.at[which, k, rows_of(h)], sem, rsem, dev).start()
-
-    def own(h, first):
-        part = zz.at[1, p, rows_of(h)]
-
-        @pl.when(q < 3)
-        def _():
-            to_line(part, q, h, TO_RIGHT, right)
-            if first is not None:
-                pl.when(first)(lambda: to_line_mask(mm.at[1, p], q, TO_RIGHT, right))
-
-        @pl.when(q > 0)
-        def _():
-            to_line(part, q, h, TO_LEFT, left)
-            if first is not None:
-                pl.when(first)(lambda: to_line_mask(mm.at[1, p], q, TO_LEFT, left))
-        plane(part, 1, p, h, sp.at[0], rb.at[p, h], {'px': mirror})
-        plane(part, 1, p, h, sp.at[1], rb.at[p, h], {'px': partner})
-        if first is not None:
-            @pl.when(first)
-            def _():
-                remote(mm.at[1, p], mm.at[1, p], spm.at[0], rmb.at[p], {'px': mirror}).start()
-                remote(mm.at[1, p], mm.at[1, p], spm.at[1], rmb.at[p], {'px': partner}).start()
-
-    mm[1, p] = mask_ref[...]
-    load.wait()
-
-    @pl.loop(0, chunks)
-    def _(h):
-        for r in range(ROWS):
-            i = h * ROWS + r
-            zt = a_ref[i, 0:128, :].astype(F32)
-            zz[1, p, i] = norm_major(zt, li_ref[0], li_ref[1]).astype(BF16)
-
-        @pl.when(h > 0)
-        def _():
-            own(h - 1, h == 1)
+            z1 = value.astype(BF16)
+            a_ref[i, 128:256, :] = z1
+            zz[1, p, i] = norm_major(z1.astype(F32), li_refs[1, 0], li_refs[1, 1]).astype(BF16)
+        finish_rows(n, x_ref, lambda i: a_ref[i, 128:256, :], lambda i: zz[0, q, i], w_ref, b_ref, wo_ref, bo_ref, lo_ref, stage8, emit)
+
+        @pl.when(jnp.logical_and(n > 1, lax.rem(n, 2) == 0))
+        def _():
+            own_line(lax.div(n, 2) - 1, n == 2)
+
+    save = pltpu.make_async_copy(a_ref.at[:, 128:256, :], keep, io.at[0])
+    save.start()
+
+    w_ref, b_ref, wo_ref, bo_ref, lo_ref = (r.at[1] for r in (w_refs, b_refs, wo_refs, bo_refs, lo_refs))
 
     @pl.loop(0, 128)
     def _(c):
         x_ref[c] = jnp.zeros((128, 128), F32)
 
-    own(jnp.int32(chunks - 1), None)
+    own_line(jnp.int32(chunks - 1), jnp.bool_(False))
+    save.wait()
+    for k in range(4):
+        def drain0(kind, when):
+            @pl.when(when)
+            def _():
+                landed(zz.at[0, k], ss1.at[kind, k])
+                landed(mb.at[0, k], sm1.at[kind, k])
+        drain0(TO_RIGHT, jnp.logical_and(q < 3, k <= q))
+        drain0(TO_LEFT, jnp.logical_and(q > 0, k >= q))
+        drain0(TO_MIRROR, diag)
+        drain0(TO_PARTNER, diag)
+    for peer in plane_peers:
+        pl.semaphore_signal(free.at[1], inc=1, device_id={'px': peer}, device_id_type=MESH)
+    pl.semaphore_wait(free.at[1], 3)
 
     def pass_on(s, m, h):
         landed(col.at[m, rows_of(h)], rc.at[m, h])
@@ -375,13 +371,13 @@
                     x_ref[c] += lax.dot_general(a_ref[c], bb_ref[c], (((0,), (0,)), ((), ())), preferred_element_type=F32)
 
     third = 3 - 3 * lax.div(q, 2)
-    second = 2 - lax.div(q, 2)
+    second = q + 1 - 2 * lax.rem(q, 2)
     last = p == third
     slot = jnp.where(p == second, 3, 2)
 
     @pl.loop(1, 4)
     def _(s):
-        m = near_order(q, s)
+        m = near_order(q, s, 1)
         lag = jnp.where(last, 2, 0)
         when = jnp.where(last, 3, slot)
 
@@ -395,6 +391,15 @@
             def _():
                 compute(h - lag)
 
+        @pl.when(jnp.logical_and(s == 1, lax.rem(q, 3) > 0))
+        def _():
+            to_line_mask(mm.at[1, p], q, 2 - q, {'py': 3 * (q - 1)})
+
+            @pl.loop(0, chunks)
+            def _(h):
+                to_line(zz.at[1, p, rows_of(h)], q, h, 2 - q, {'py': 3 * (q - 1)})
+
+    load = pltpu.make_async_copy(keep, a_ref.at[:, 0:128, :], io.at[0])
     load.start()
     load.wait()
 
@@ -426,15 +431,28 @@
     pltpu.make_async_copy(bb_ref.at[:, 0:128, :], out_ref, io.at[1]).wait()
 
 
-def incoming(z, mask, wt, bias, ln_in, wo, bo, ln_out):
+VM = pl.BlockSpec(memory_space=pltpu.VMEM)
+ANY = pl.BlockSpec(memory_space=pl.ANY)
+DMA = pltpu.SemaphoreType.DMA
+
+
+def both_updates(*args):
     n = 128 // ROWS
+    block = jax.ShapeDtypeStruct((128, 128, 128), BF16)
     return pl.pallas_call(
-        incoming_kernel,
-        out_shape=[jax.ShapeDtypeStruct((128, 128, 128), BF16), jax.ShapeDtypeStruct((4, 128, 128, 128), BF16)],
+        kernel,
+        out_shape=[block, jax.ShapeDtypeStruct((4, 128, 128, 128), BF16), block],
         in_specs=[ANY] + [VM] * 7,
-        out_specs=[ANY, ANY],
+        out_specs=[ANY, ANY, ANY],
         scratch_shapes=[
+            pltpu.VMEM((2, 640, 128), BF16),
+            pltpu.VMEM((2, 640, 128), F32),
+            pltpu.VMEM((2, 2, 128, 128), F32),
+            pltpu.VMEM((2, 128, 128), BF16),
+            pltpu.VMEM((2, 128, 128), F32),
+            pltpu.VMEM((2, 2, 128, 128), F32),
             pltpu.VMEM((2, 4, 128, 128, 128), BF16),
+            pltpu.VMEM((2, 4, 128, 128), BF16),
             pltpu.VMEM((2, 4, 128, 128), BF16),
             pltpu.VMEM((4, 128, 128), BF16),
             pltpu.VMEM((128, 256, 128), BF16),
@@ -442,12 +460,14 @@
             pltpu.VMEM((128, 128, 128), F32),
             pltpu.VMEM((ROWS, 128, 128), F32),
             pltpu.VMEM((8, 128, 128), F32),
+            DMA((4, n)), DMA((4, n)), DMA((4,)), DMA((4,)), DMA((4, 4)), DMA((4, 4)),
             DMA((4, n)), DMA((4, n)), DMA((4, n)), DMA((n,)), DMA((4,)), DMA((4,)), DMA((4,)), DMA((2,)),
             DMA((3, 4)), DMA((3, 4)), DMA((3,)), DMA((3,)),
+            pltpu.SemaphoreType.REGULAR((2,)),
         ],
-        compiler_params=pltpu.CompilerParams(collective_id=1, has_side_effects=True, vmem_limit_bytes=67043328),
-        name='incoming',
-    )(z, mask, wt, bias, ln_in, wo, bo, ln_out)[0]
+        compiler_params=pltpu.CompilerParams(collective_id=0, has_side_effects=True, vmem_limit_bytes=67043328),
+        name='both_updates',
+    )(*args)[0]
 
 
 def solution(mesh):
@@ -455,14 +475,4 @@
     mask_spec = P(('batch', 'px'), 'py')
     whole = P()
 
-    def device_body(pair_blk, mask_blk, ln_in, w_in, b_in, ln_out, w_out, b_out):
-        mask = mask_blk.astype(BF16)
-        wt = jnp.swapaxes(w_in, 1, 2)
-        wo = jnp.swapaxes(w_out, 1, 2)
-        def wide(v):
-            return jnp.broadcast_to(v.astype(F32)[..., None], v.shape + (128,))
-        bias, bo, li, lo = wide(b_in), wide(b_out), wide(ln_in), wide(ln_out)
-        z1 = outgoing(pair_blk, mask, wt[0], bias[0], li[0], wo[0], bo[0], lo[0])
-        return incoming(z1, mask, wt[1], bias[1], li[1], wo[1], bo[1], lo[1])
-
-    return jax.shard_map(device_body, mesh=mesh, in_specs=(pair_spec, mask_spec, whole, whole, whole, whole, whole, whole), out_specs=pair_spec, check_vma=False)
+    return jax.shard_map(both_updates, mesh=mesh, in_specs=(pair_spec, mask_spec, whole, whole, whole, whole, whole, whole), out_specs=pair_spec, check_vma=False)

time: 651 us -> 611 us (0.939)
  Pallas kernels: 632 us -> 605 us
  local copies, waits for them, and re-layouts: 14.5 us -> 4.79 us
    pallas_call x2 -> x1, Pallas kernels: 632 us -> 605 us  [both_updates(): pl.pallas_call(kernel, out_shape=[block, jax.ShapeDtypeStruct((4, 128, 12...]
where the time goes in v3:
time: 611 us; the launch traced here: 610 us
  Pallas kernels  605 us (99%)
    pallas_call x1, Pallas kernels, both_updates(): pl.pallas_call(kernel, out_shape=[block, jax.ShapeDtypeStruct((4, 128, 12...  605 us

profile of v3, /device:TPU:26, one launch (start us, length us, event | category | flops | bytes accessed | tf_op | source)
XLA Modules:
  0.0 609.9 jit_solution(7326792007476667614)
XLA Ops:
  0.0 605.1 %both_updates.1 = (bf16[128,128,128]{2,1,0:T(8,128)(2,1)}, bf16[4,128,128,128]{3,2,1,0:T(8,128)(2,1)}, bf16[128,128,128]{2,1,0:T(8,128)(2,1)}) custom-call(bf16[128,128,128]{2,1,0:T(8,128)(2,1)} %z_ref.1, s32[128,128]{1,0:T(8,128)} %mask_ref.1, bf16[2,2,128]{2,1,0:T(2,128)(2,1)} %li_in.1, bf16[2,128,640]{2,1,0:T(8,128)(2,1)} %w_in.1, bf16[2,640]{1,0:T(2,128)(2,1)} %b_in.1, ...), custom_call_target="tpu_custom_call" | custom-call | tf_op jit(solution)/shard_map/both_updates/pallas_call | solution.py:442
  605.1 4.8 copy.10

commit v4 on v3

--- a/solution.py
+++ b/solution.py
@@ -42,14 +42,15 @@
 
 
 def finish_rows(n, x_ref, z_row, zn_row, w_ref, b_ref, wo_ref, bo_ref, lo_ref, stage, emit):
-    i0 = pl.multiple_of(n * 8, 8)
-    x = x_ref[:, pl.ds(i0, 8), :]
-    average = jnp.mean(x, axis=0)
-    centered = x - average[None]
-    variance = jnp.mean(centered * centered, axis=0)
-    scale = lax.rsqrt(variance + LN_EPS)
-    stage[...] = jnp.transpose(centered * scale[None], (1, 0, 2))
-    for r in range(0, 8, 2):
+    i0 = pl.multiple_of(n * ROWS, ROWS)
+    for r in range(0, ROWS, 8):
+        x = x_ref[:, pl.ds(i0 + r, 8), :]
+        average = jnp.mean(x, axis=0)
+        centered = x - average[None]
+        variance = jnp.mean(centered * centered, axis=0)
+        scale = lax.rsqrt(variance + LN_EPS)
+        stage[r:r + 8] = jnp.transpose(centered * scale[None], (1, 0, 2))
+    for r in range(0, ROWS, 2):
         pair = [(stage[r + t] * lo_ref[0] + lo_ref[1]).astype(BF16) for t in range(2)]
         update = jnp.dot(wo_ref[...], jnp.concatenate(pair, axis=1), preferred_element_type=F32)
         zn = jnp.concatenate([zn_row(i0 + r), zn_row(i0 + r + 1)], axis=1)
@@ -85,11 +86,11 @@
         pl.semaphore_signal(barrier, inc=1, device_id={'py': q - 1}, device_id_type=MESH)
 
     edge = jnp.int32(1) * (q == 0) + jnp.int32(1) * (q == 3)
-    pl.semaphore_wait(barrier, len(peers) + 2 - edge)
+    return lambda: pl.semaphore_wait(barrier, len(peers) + 2 - edge)
 
 
 def kernel(z_ref, mask_ref, li_in, w_in, b_in, lo_in, wo_in, bo_in, out_ref, col, keep,
-           w_refs, b_refs, li_refs, wo_refs, bo_refs, lo_refs, zz, mb, mm, mc, a_ref, bb_ref, x_ref, stage, stage8,
+           w_refs, b_refs, li_refs, wo_refs, bo_refs, lo_refs, zz, mb, mm, mc, a_ref, bb_ref, x_ref, stage,
            ra1, rb1, rma1, rmb1, ss1, sm1, rc, ra, rb, lc, rmc, rma, rmb, io, ss, sm, sp, spm, free):
     chunks = 128 // ROWS
     p, q = lax.axis_index('px'), lax.axis_index('py')
@@ -102,9 +103,11 @@
     bsel = 1 - asel
     plane_peers = [lax.rem(p + d, 4) for d in (1, 2, 3)]
 
-    greet(p, q, True)
-    load = pltpu.make_async_copy(z_ref, bb_ref.at[:, 128:256, :], io.at[0])
-    load.start()
+    met = greet(p, q, True)
+    load_first = pltpu.make_async_copy(z_ref.at[0:ROWS], bb_ref.at[0:ROWS, 128:256, :], io.at[0])
+    load_rest = pltpu.make_async_copy(z_ref.at[ROWS:128], bb_ref.at[ROWS:128, 128:256, :], io.at[1])
+    load_first.start()
+    load_rest.start()
 
     def rows_of(h):
         return pl.ds(pl.multiple_of(h * ROWS, ROWS), ROWS)
@@ -159,19 +162,22 @@
         ln_rows = li_in[u].astype(F32)
         for t in range(2):
             li_refs[u, t] = wide(ln_rows[t:t + 1])
-    load.wait()
-
-    @pl.loop(0, chunks)
-    def _(h):
+    def prepare(h):
         for r in range(ROWS):
             i = h * ROWS + r
             zt = jnp.transpose(bb_ref[i, 128:256, :].astype(F32))
             a_ref[i, 128:256, :] = zt.astype(BF16)
             zb[0, q, i] = norm_major(zt, li_ref[0], li_ref[1]).astype(BF16)
 
-        @pl.when(h > 0)
-        def _():
-            spread(q, h - 1, h == 1)
+    load_first.wait()
+    prepare(0)
+    met()
+    load_rest.wait()
+
+    @pl.loop(1, chunks)
+    def _(h):
+        prepare(h)
+        spread(q, h - 1, h == 1)
 
     @pl.loop(0, 128)
     def _(c):
@@ -262,17 +268,17 @@
     for peer in plane_peers:
         pl.semaphore_signal(free.at[0], inc=1, device_id={'px': peer}, device_id_type=MESH)
 
-    @pl.loop(0, 16)
+    @pl.loop(0, chunks)
     def _(n):
         def emit(i, value):
             z1 = value.astype(BF16)
             a_ref[i, 128:256, :] = z1
             zz[1, p, i] = norm_major(z1.astype(F32), li_refs[1, 0], li_refs[1, 1]).astype(BF16)
-        finish_rows(n, x_ref, lambda i: a_ref[i, 128:256, :], lambda i: zz[0, q, i], w_ref, b_ref, wo_ref, bo_ref, lo_ref, stage8, emit)
-
-        @pl.when(jnp.logical_and(n > 1, lax.rem(n, 2) == 0))
-        def _():
-            own_line(lax.div(n, 2) - 1, n == 2)
+        finish_rows(n, x_ref, lambda i: a_ref[i, 128:256, :], lambda i: zz[0, q, i], w_ref, b_ref, wo_ref, bo_ref, lo_ref, stage, emit)
+
+        @pl.when(n > 0)
+        def _():
+            own_line(n - 1, n == 1)
 
     save = pltpu.make_async_copy(a_ref.at[:, 128:256, :], keep, io.at[0])
     save.start()
@@ -284,6 +290,25 @@
         x_ref[c] = jnp.zeros((128, 128), F32)
 
     own_line(jnp.int32(chunks - 1), jnp.bool_(False))
+    inner = lax.rem(q, 3) > 0
+
+    @pl.when(inner)
+    def _():
+        m = near_order(q, jnp.int32(1), 1)
+        kind, outer = 2 - q, {'py': 3 * (q - 1)}
+        landed(mc.at[m], rmc.at[m])
+        to_line_mask(mc.at[m], m, kind, outer)
+
+        @pl.loop(0, chunks)
+        def _(h):
+            landed(col.at[m, rows_of(h)], rc.at[m, h])
+            to_line(col.at[m, rows_of(h)], m, h, kind, outer)
+        to_line_mask(mm.at[1, p], q, kind, outer)
+
+        @pl.loop(0, chunks)
+        def _(h):
+            to_line(zz.at[1, p, rows_of(h)], q, h, kind, outer)
+
     save.wait()
     for k in range(4):
         def drain0(kind, when):
@@ -300,16 +325,18 @@
     pl.semaphore_wait(free.at[1], 3)
 
     def pass_on(s, m, h):
-        landed(col.at[m, rows_of(h)], rc.at[m, h])
-        pl.when(h == 0)(lambda: landed(mc.at[m], rmc.at[m]))
+        @pl.when(jnp.logical_or(s > 1, lax.rem(q, 3) == 0))
+        def _():
+            landed(col.at[m, rows_of(h)], rc.at[m, h])
+            pl.when(h == 0)(lambda: landed(mc.at[m], rmc.at[m]))
         part = col.at[m, rows_of(h)]
 
-        @pl.when(jnp.logical_and(q < 3, m < q))
+        @pl.when(jnp.logical_and(s > 1, jnp.logical_and(q < 3, m < q)))
         def _():
             to_line(part, m, h, TO_RIGHT, right)
             pl.when(h == 0)(lambda: to_line_mask(mc.at[m], m, TO_RIGHT, right))
 
-        @pl.when(jnp.logical_and(q > 0, m > q))
+        @pl.when(jnp.logical_and(s > 1, jnp.logical_and(q > 0, m > q)))
         def _():
             to_line(part, m, h, TO_LEFT, left)
             pl.when(h == 0)(lambda: to_line_mask(mc.at[m], m, TO_LEFT, left))
@@ -337,16 +364,28 @@
                 landed(mm.at[1, mirror], rmb.at[mirror])
                 remote(mm.at[1, mirror], mm.at[1, mirror], spm.at[2], rmb.at[mirror], {'px': partner}).start()
 
+    def group_row(k, h):
+        return pl.multiple_of(lax.rem(h, 4) * 64 + k * ROWS, ROWS)
+
     def compute(h):
+        @pl.when(lax.rem(h, 4) == 0)
+        def _():
+            @pl.loop(0, 16)
+            def _(t):
+                k, g = lax.div(t, 4), h + lax.rem(t, 4)
+                r0 = pl.multiple_of(g * ROWS, ROWS)
+
+                @pl.when(jnp.logical_and(k != p, k != mirror))
+                def _():
+                    landed(zz.at[1, k, rows_of(g)], rb.at[k, g])
+                    pl.when(g == 0)(lambda: landed(mm.at[1, k], rmb.at[k]))
+                mask_b = mm[1, k, pl.ds(r0, ROWS), :].astype(F32)
+                project(lambda r: zz[1, k, r0 + r], mask_b, w_ref, b_ref, 256, stage, bb_ref, group_row(k, g))
+
         r0 = pl.multiple_of(h * ROWS, ROWS)
 
         @pl.loop(0, 4)
         def _(k):
-            @pl.when(jnp.logical_and(k != p, k != mirror))
-            def _():
-                landed(zz.at[1, k, rows_of(h)], rb.at[k, h])
-                pl.when(h == 0)(lambda: landed(mm.at[1, k], rmb.at[k]))
-
             @pl.when(jnp.logical_and(off_diag, k != p))
             def _():
                 landed(zz.at[0, k, rows_of(h)], ra.at[k, h])
@@ -355,20 +394,17 @@
             @pl.when(jnp.logical_and(off_diag, k == p))
             def _():
                 landed(zz.at[0, k, rows_of(h)], lc.at[h])
-
-            at = pl.multiple_of(k * 64 + lax.rem(h, 4) * ROWS, ROWS)
-            mask_b = mm[1, k, pl.ds(r0, ROWS), :].astype(F32)
-            project(lambda r: zz[1, k, r0 + r], mask_b, w_ref, b_ref, 256, stage, bb_ref, at)
             mask_a = mm[asel, k, pl.ds(r0, ROWS), :].astype(F32)
-            project(lambda r: zz[asel, k, r0 + r], mask_a, w_ref, b_ref, 0, stage, a_ref, at)
-
-        @pl.when(lax.rem(h, 4) == 3)
-        def _():
-            @pl.loop(0, 128 // 8)
-            def _(n):
-                for u in range(8):
-                    c = n * 8 + u
-                    x_ref[c] += lax.dot_general(a_ref[c], bb_ref[c], (((0,), (0,)), ((), ())), preferred_element_type=F32)
+            project(lambda r: zz[asel, k, r0 + r], mask_a, w_ref, b_ref, 0, stage, a_ref, group_row(k, h))
+
+        for at, first, last_row in ((3, 0, 256), (6, 0, 192), (7, 192, 256)):
+            @pl.when(h == at)
+            def _():
+                @pl.loop(0, 128 // 8)
+                def _(n):
+                    for u in range(8):
+                        c = n * 8 + u
+                        x_ref[c] += lax.dot_general(a_ref[c, first:last_row, :], bb_ref[c, first:last_row, :], (((0,), (0,)), ((), ())), preferred_element_type=F32)
 
     third = 3 - 3 * lax.div(q, 2)
     second = q + 1 - 2 * lax.rem(q, 2)
@@ -391,30 +427,22 @@
             def _():
                 compute(h - lag)
 
-        @pl.when(jnp.logical_and(s == 1, lax.rem(q, 3) > 0))
-        def _():
-            to_line_mask(mm.at[1, p], q, 2 - q, {'py': 3 * (q - 1)})
-
-            @pl.loop(0, chunks)
-            def _(h):
-                to_line(zz.at[1, p, rows_of(h)], q, h, 2 - q, {'py': 3 * (q - 1)})
-
     load = pltpu.make_async_copy(keep, a_ref.at[:, 0:128, :], io.at[0])
     load.start()
     load.wait()
 
     def store(n):
-        rows = pl.ds(pl.multiple_of(n * 8, 8), 8)
+        rows = rows_of(n)
         return pltpu.make_async_copy(bb_ref.at[rows, 0:128, :], out_ref.at[rows], io.at[1])
 
-    @pl.loop(0, 16)
+    @pl.loop(0, chunks)
     def _(n):
         def emit(i, value):
-            bb_ref[i, 0:128, :] = jnp.transpose(value).astype(BF16)
-        finish_rows(n, x_ref, lambda i: a_ref[i, 0:128, :], lambda i: zz[1, p, i], w_ref, b_ref, wo_ref, bo_ref, lo_ref, stage8, emit)
+            bb_ref[i, 0:128, :] = jnp.transpose(value.astype(BF16))
+        finish_rows(n, x_ref, lambda i: a_ref[i, 0:128, :], lambda i: zz[1, p, i], w_ref, b_ref, wo_ref, bo_ref, lo_ref, stage, emit)
         pl.when(n > 0)(lambda: store(n - 1).start())
 
-    store(jnp.int32(15)).start()
+    store(jnp.int32(chunks - 1)).start()
 
     for m in range(4):
         def drain(kind, when):
@@ -459,7 +487,6 @@
             pltpu.VMEM((128, 256, 128), BF16),
             pltpu.VMEM((128, 128, 128), F32),
             pltpu.VMEM((ROWS, 128, 128), F32),
-            pltpu.VMEM((8, 128, 128), F32),
             DMA((4, n)), DMA((4, n)), DMA((4,)), DMA((4,)), DMA((4, 4)), DMA((4, 4)),
             DMA((4, n)), DMA((4, n)), DMA((4, n)), DMA((n,)), DMA((4,)), DMA((4,)), DMA((4,)), DMA((2,)),
             DMA((3, 4)), DMA((3, 4)), DMA((3,)), DMA((3,)),

time: 611 us -> 602 us (0.985)
  Pallas kernels: 605 us -> 597 us
    pallas_call x1, Pallas kernels: 605 us -> 597 us  [both_updates(): pl.pallas_call(kernel, out_shape=[block, jax.ShapeDtypeStruct((4, 128, 12...]
where the time goes in v4:
time: 602 us
  Pallas kernels  597 us (99%)
    pallas_call x1, Pallas kernels, both_updates(): pl.pallas_call(kernel, out_shape=[block, jax.ShapeDtypeStruct((4, 128, 12...  597 us

profile of v4, /device:TPU:26, one launch (start us, length us, event | category | flops | bytes accessed | tf_op | source)
XLA Modules:
  0.0 601.8 jit_solution(16324610842200147578)
XLA Ops:
  0.0 597.0 %both_updates.1 = (bf16[128,128,128]{2,1,0:T(8,128)(2,1)}, bf16[4,128,128,128]{3,2,1,0:T(8,128)(2,1)}, bf16[128,128,128]{2,1,0:T(8,128)(2,1)}) custom-call(bf16[128,128,128]{2,1,0:T(8,128)(2,1)} %z_ref.1, s32[128,128]{1,0:T(8,128)} %mask_ref.1, bf16[2,2,128]{2,1,0:T(2,128)(2,1)} %li_in.1, bf16[2,128,640]{2,1,0:T(8,128)(2,1)} %w_in.1, bf16[2,640]{1,0:T(2,128)(2,1)} %b_in.1, ...), custom_call_target="tpu_custom_call" | custom-call | tf_op jit(solution)/shard_map/both_updates/pallas_call | solution.py:470
  597.0 4.8 copy.10

commit v5 on v4

--- a/solution.py
+++ b/solution.py
@@ -10,7 +10,7 @@
 LN_EPS = 1e-5
 MESH = pl.DeviceIdType.MESH
 F32, BF16 = jnp.float32, jnp.bfloat16
-ROWS = 16
+ROWS, HALF = 16, 8
 TO_RIGHT, TO_LEFT, TO_PARTNER, TO_MIRROR = 0, 1, 2, 3
 
 
@@ -230,8 +230,11 @@
                 c = n * 16 + u
                 x_ref[c] += lax.dot_general(a_ref[c, 0:128, :], bb_ref[c, 0:128, :], (((1,), (1,)), ((), ())), preferred_element_type=F32)
 
-    def to_line(src, m, h, kind, dev):
-        remote(src, col.at[m, rows_of(h)], ss.at[kind, m], rc.at[m, h], dev).start()
+    def half_rows(t):
+        return pl.ds(pl.multiple_of(t * HALF, HALF), HALF)
+
+    def to_line(src, m, t, kind, dev):
+        remote(src, col.at[m, half_rows(t)], ss.at[kind, m], rc.at[m, t], dev).start()
 
     def to_line_mask(src, m, kind, dev):
         remote(src, mc.at[m], sm.at[kind, m], rmc.at[m], dev).start()
@@ -244,12 +247,14 @@
 
         @pl.when(jnp.logical_and(q < 3, q != 2))
         def _():
-            to_line(part, q, h, TO_RIGHT, right)
+            for t in (2 * h, 2 * h + 1):
+                to_line(zz.at[1, p, half_rows(t)], q, t, TO_RIGHT, right)
             pl.when(first)(lambda: to_line_mask(mm.at[1, p], q, TO_RIGHT, right))
 
         @pl.when(jnp.logical_and(q > 0, q != 1))
         def _():
-            to_line(part, q, h, TO_LEFT, left)
+            for t in (2 * h, 2 * h + 1):
+                to_line(zz.at[1, p, half_rows(t)], q, t, TO_LEFT, left)
             pl.when(first)(lambda: to_line_mask(mm.at[1, p], q, TO_LEFT, left))
 
         @pl.when(first)
@@ -299,15 +304,15 @@
         landed(mc.at[m], rmc.at[m])
         to_line_mask(mc.at[m], m, kind, outer)
 
-        @pl.loop(0, chunks)
-        def _(h):
-            landed(col.at[m, rows_of(h)], rc.at[m, h])
-            to_line(col.at[m, rows_of(h)], m, h, kind, outer)
+        @pl.loop(0, 2 * chunks)
+        def _(t):
+            landed(col.at[m, half_rows(t)], rc.at[m, t])
+            to_line(col.at[m, half_rows(t)], m, t, kind, outer)
         to_line_mask(mm.at[1, p], q, kind, outer)
 
-        @pl.loop(0, chunks)
-        def _(h):
-            to_line(zz.at[1, p, rows_of(h)], q, h, kind, outer)
+        @pl.loop(0, 2 * chunks)
+        def _(t):
+            to_line(zz.at[1, p, half_rows(t)], q, t, kind, outer)
 
     save.wait()
     for k in range(4):
@@ -324,38 +329,39 @@
         pl.semaphore_signal(free.at[1], inc=1, device_id={'px': peer}, device_id_type=MESH)
     pl.semaphore_wait(free.at[1], 3)
 
-    def pass_on(s, m, h):
+    def pass_on(s, m, t):
         @pl.when(jnp.logical_or(s > 1, lax.rem(q, 3) == 0))
         def _():
-            landed(col.at[m, rows_of(h)], rc.at[m, h])
-            pl.when(h == 0)(lambda: landed(mc.at[m], rmc.at[m]))
-        part = col.at[m, rows_of(h)]
+            landed(col.at[m, half_rows(t)], rc.at[m, t])
+            pl.when(t == 0)(lambda: landed(mc.at[m], rmc.at[m]))
+        part = col.at[m, half_rows(t)]
 
         @pl.when(jnp.logical_and(s > 1, jnp.logical_and(q < 3, m < q)))
         def _():
-            to_line(part, m, h, TO_RIGHT, right)
-            pl.when(h == 0)(lambda: to_line_mask(mc.at[m], m, TO_RIGHT, right))
+            to_line(part, m, t, TO_RIGHT, right)
+            pl.when(t == 0)(lambda: to_line_mask(mc.at[m], m, TO_RIGHT, right))
 
         @pl.when(jnp.logical_and(s > 1, jnp.logical_and(q > 0, m > q)))
         def _():
-            to_line(part, m, h, TO_LEFT, left)
-            pl.when(h == 0)(lambda: to_line_mask(mc.at[m], m, TO_LEFT, left))
+            to_line(part, m, t, TO_LEFT, left)
+            pl.when(t == 0)(lambda: to_line_mask(mc.at[m], m, TO_LEFT, left))
 
         @pl.when(m != p)
         def _():
-            plane(part, 0, p, h, ss.at[2, m], ra.at[p, h], {'px': m})
-            pl.when(h == 0)(lambda: remote(mc.at[m], mm.at[0, p], sm.at[2, m], rma.at[p], {'px': m}).start())
+            remote(part, zz.at[0, p, half_rows(t)], ss.at[2, m], ra.at[p, t], {'px': m}).start()
+            pl.when(t == 0)(lambda: remote(mc.at[m], mm.at[0, p], sm.at[2, m], rma.at[p], {'px': m}).start())
 
         @pl.when(m == p)
         def _():
-            pltpu.make_async_copy(part, zz.at[0, p, rows_of(h)], lc.at[h]).start()
-
-            @pl.when(h == 0)
+            pltpu.make_async_copy(part, zz.at[0, p, half_rows(t)], lc.at[t]).start()
+
+            @pl.when(t == 0)
             def _():
                 mm[0, p] = mc[p]
 
-        @pl.when(s == 1)
-        def _():
+        @pl.when(jnp.logical_and(s == 1, lax.rem(t, 2) == 1))
+        def _():
+            h = lax.div(t, 2)
             landed(zz.at[1, mirror, rows_of(h)], rb.at[mirror, h])
             plane(zz.at[1, mirror, rows_of(h)], 1, mirror, h, sp.at[2], rb.at[mirror, h], {'px': partner})
 
@@ -388,14 +394,21 @@
         def _(k):
             @pl.when(jnp.logical_and(off_diag, k != p))
             def _():
-                landed(zz.at[0, k, rows_of(h)], ra.at[k, h])
+                for t in (2 * h, 2 * h + 1):
+                    landed(zz.at[0, k, half_rows(t)], ra.at[k, t])
                 pl.when(h == 0)(lambda: landed(mm.at[0, k], rma.at[k]))
 
             @pl.when(jnp.logical_and(off_diag, k == p))
             def _():
-                landed(zz.at[0, k, rows_of(h)], lc.at[h])
+                for t in (2 * h, 2 * h + 1):
+                    landed(zz.at[0, k, half_rows(t)], lc.at[t])
             mask_a = mm[asel, k, pl.ds(r0, ROWS), :].astype(F32)
             project(lambda r: zz[asel, k, r0 + r], mask_a, w_ref, b_ref, 0, stage, a_ref, group_row(k, h))
+
+        @pl.when(h == 7)
+        def _():
+            landed(zz.at[1, 0], sp.at[2])
+            pltpu.make_async_copy(keep, zz.at[1, mirror], io.at[0]).start()
 
         for at, first, last_row in ((3, 0, 256), (6, 0, 192), (7, 192, 256)):
             @pl.when(h == at)
@@ -414,22 +427,19 @@
     @pl.loop(1, 4)
     def _(s):
         m = near_order(q, s, 1)
-        lag = jnp.where(last, 2, 0)
         when = jnp.where(last, 3, slot)
 
-        @pl.loop(0, chunks + 2 * lax.div(s, 3))
+        @pl.loop(0, chunks)
         def _(h):
-            @pl.when(h < chunks)
-            def _():
-                pass_on(s, m, h)
-
-            @pl.when(jnp.logical_and(s == when, jnp.logical_and(h >= lag, h < chunks + lag)))
-            def _():
-                compute(h - lag)
-
-    load = pltpu.make_async_copy(keep, a_ref.at[:, 0:128, :], io.at[0])
-    load.start()
-    load.wait()
+            @pl.loop(0, 2)
+            def _(t):
+                pass_on(s, m, 2 * h + t)
+
+            @pl.when(s == when)
+            def _():
+                compute(h)
+
+    pltpu.make_async_copy(keep, zz.at[1, mirror], io.at[0]).wait()
 
     def store(n):
         rows = rows_of(n)
@@ -439,7 +449,7 @@
     def _(n):
         def emit(i, value):
             bb_ref[i, 0:128, :] = jnp.transpose(value.astype(BF16))
-        finish_rows(n, x_ref, lambda i: a_ref[i, 0:128, :], lambda i: zz[1, p, i], w_ref, b_ref, wo_ref, bo_ref, lo_ref, stage, emit)
+        finish_rows(n, x_ref, lambda i: zz[1, mirror, i], lambda i: zz[1, p, i], w_ref, b_ref, wo_ref, bo_ref, lo_ref, stage, emit)
         pl.when(n > 0)(lambda: store(n - 1).start())
 
     store(jnp.int32(chunks - 1)).start()
@@ -454,7 +464,8 @@
         drain(TO_LEFT, jnp.logical_and(q > 0, m >= q))
         drain(2, jnp.logical_and(m != q, m != p))
     for kind in range(3):
-        landed(zz.at[1, 0], sp.at[kind])
+        if kind < 2:
+            landed(zz.at[1, 0], sp.at[kind])
         landed(mm.at[1, 0], spm.at[kind])
     pltpu.make_async_copy(bb_ref.at[:, 0:128, :], out_ref, io.at[1]).wait()
 
@@ -488,7 +499,7 @@
             pltpu.VMEM((128, 128, 128), F32),
             pltpu.VMEM((ROWS, 128, 128), F32),
             DMA((4, n)), DMA((4, n)), DMA((4,)), DMA((4,)), DMA((4, 4)), DMA((4, 4)),
-            DMA((4, n)), DMA((4, n)), DMA((4, n)), DMA((n,)), DMA((4,)), DMA((4,)), DMA((4,)), DMA((2,)),
+            DMA((4, 2 * n)), DMA((4, 2 * n)), DMA((4, n)), DMA((2 * n,)), DMA((4,)), DMA((4,)), DMA((4,)), DMA((2,)),
             DMA((3, 4)), DMA((3, 4)), DMA((3,)), DMA((3,)),
             pltpu.SemaphoreType.REGULAR((2,)),
         ],

time: 602 us -> 599 us (level)
  no operation moved by 1% of the time
where the time goes in v5:
time: 599 us
  Pallas kernels  594 us (99%)
    pallas_call x1, Pallas kernels, both_updates(): pl.pallas_call(kernel, out_shape=[block, jax.ShapeDtypeStruct((4, 128, 12...  594 us

profile of v5, /device:TPU:26, one launch (start us, length us, event | category | flops | bytes accessed | tf_op | source)
XLA Modules:
  0.0 599.0 jit_solution(7599290766937408851)
XLA Ops:
  0.0 594.2 %both_updates.1 = (bf16[128,128,128]{2,1,0:T(8,128)(2,1)}, bf16[4,128,128,128]{3,2,1,0:T(8,128)(2,1)}, bf16[128,128,128]{2,1,0:T(8,128)(2,1)}) custom-call(bf16[128,128,128]{2,1,0:T(8,128)(2,1)} %z_ref.1, s32[128,128]{1,0:T(8,128)} %mask_ref.1, bf16[2,2,128]{2,1,0:T(2,128)(2,1)} %li_in.1, bf16[2,128,640]{2,1,0:T(8,128)(2,1)} %w_in.1, bf16[2,640]{1,0:T(2,128)(2,1)} %b_in.1, ...), custom_call_target="tpu_custom_call" | custom-call | tf_op jit(solution)/shard_map/both_updates/pallas_call | solution.py:481
  594.2 4.8 copy.10

commit v6 on v5

--- a/solution.py
+++ b/solution.py
@@ -413,10 +413,10 @@
         for at, first, last_row in ((3, 0, 256), (6, 0, 192), (7, 192, 256)):
             @pl.when(h == at)
             def _():
-                @pl.loop(0, 128 // 8)
+                @pl.loop(0, 128 // 16)
                 def _(n):
-                    for u in range(8):
-                        c = n * 8 + u
+                    for u in range(16):
+                        c = n * 16 + u
                         x_ref[c] += lax.dot_general(a_ref[c, first:last_row, :], bb_ref[c, first:last_row, :], (((0,), (0,)), ((), ())), preferred_element_type=F32)
 
     third = 3 - 3 * lax.div(q, 2)

time: 599 us -> 598 us (level)
  no operation moved by 1% of the time
where the time goes in v6:
time: 598 us; the launch traced here: 597 us
  Pallas kernels  593 us (99%)
    pallas_call x1, Pallas kernels, both_updates(): pl.pallas_call(kernel, out_shape=[block, jax.ShapeDtypeStruct((4, 128, 12...  593 us

profile of v6, /device:TPU:26, one launch (start us, length us, event | category | flops | bytes accessed | tf_op | source)
XLA Modules:
  0.0 597.5 jit_solution(10975046493879573087)
XLA Ops:
  0.0 592.7 %both_updates.1 = (bf16[128,128,128]{2,1,0:T(8,128)(2,1)}, bf16[4,128,128,128]{3,2,1,0:T(8,128)(2,1)}, bf16[128,128,128]{2,1,0:T(8,128)(2,1)}) custom-call(bf16[128,128,128]{2,1,0:T(8,128)(2,1)} %z_ref.1, s32[128,128]{1,0:T(8,128)} %mask_ref.1, bf16[2,2,128]{2,1,0:T(2,128)(2,1)} %li_in.1, bf16[2,128,640]{2,1,0:T(8,128)(2,1)} %w_in.1, bf16[2,640]{1,0:T(2,128)(2,1)} %b_in.1, ...), custom_call_target="tpu_custom_call" | custom-call | tf_op jit(solution)/shard_map/both_updates/pallas_call | solution.py:481
  592.7 4.8 copy.10
